TPU v7x, 8 devices: a whole 2x2x1 slice. The times are simulated.
8 devices in a mesh: dp: 1 (over z), sp: 2 (over y), cp: 4 (over x, core).
Axes of the slice: x: 2, y: 2, z: 1, core: 2. Of those that a mesh axis runs over, the one named last changes fastest.
Arguments:
- hidden: bfloat16 [8, 2048, 4096], P('dp', ('cp', 'sp'))
- w_qkv: bfloat16 [4096, 3, 32, 128], replicated
- w_out: bfloat16 [32, 128, 4096], replicated
- norm_gain: bfloat16 [4096], replicated
- w_up: bfloat16 [4096, 16384], replicated
- b_up: bfloat16 [16384], replicated
- w_down: bfloat16 [16384, 4096], replicated
- b_down: bfloat16 [4096], replicated
Outputs:
- output: bfloat16 [8, 2048, 4096], P('dp', ('cp', 'sp'))
All inputs are finite; a program needn't handle non-finite values.
Results may differ from a plain program's by a relative error of at most 0.0103326.
Values are sent between devices in bfloat16 or wider.
A program may use at most 1.75 GiB of HBM per device.

v0:
```python
import jax
import jax.numpy as jnp
from jax import lax
from jax.sharding import PartitionSpec as P

NORM_EPS = 1e-6


def attend_step(queries, key_blk, val_blk, soft_state):
    run_max, run_sum, run_acc = soft_state
    scores = jnp.einsum("bqhd,bkhd->bhqk", queries, key_blk, preferred_element_type=jnp.float32) * (queries.shape[-1] ** -0.5)
    new_max = jnp.maximum(run_max, jnp.max(scores, axis=-1))
    rescale = jnp.exp(run_max - new_max)
    exp_scores = jnp.exp(scores - new_max[..., None])
    new_sum = run_sum * rescale + jnp.sum(exp_scores, axis=-1)
    new_acc = run_acc * rescale[..., None] + jnp.einsum("bhqk,bkhd->bhqd", exp_scores.astype(jnp.bfloat16), val_blk, preferred_element_type=jnp.float32)
    return new_max, new_sum, new_acc


def empty_state(batch_size, num_heads, q_len, head_dim):
    return (jnp.full((batch_size, num_heads, q_len), -jnp.inf, jnp.float32), jnp.zeros((batch_size, num_heads, q_len), jnp.float32), jnp.zeros((batch_size, num_heads, q_len, head_dim), jnp.float32))


def block_tail(hidden, attn_heads, w_out, norm_gain, w_up, b_up, w_down, b_down):
    attn_out = jnp.einsum("bhtd,hdc->btc", attn_heads, w_out, preferred_element_type=jnp.float32).astype(jnp.bfloat16)
    resid_wide = (hidden.astype(jnp.float32) + attn_out.astype(jnp.float32)).astype(jnp.bfloat16).astype(jnp.float32)
    inv_rms = lax.rsqrt(jnp.mean(resid_wide * resid_wide, axis=-1, keepdims=True) + NORM_EPS)
    normed = (resid_wide * inv_rms * norm_gain.astype(jnp.float32)).astype(jnp.bfloat16)
    up_proj = jnp.einsum("btc,cf->btf", normed, w_up, preferred_element_type=jnp.float32) + b_up.astype(jnp.float32)
    up_act = jax.nn.gelu(up_proj, approximate=True).astype(jnp.bfloat16)
    down_proj = jnp.einsum("btf,fc->btc", up_act, w_down, preferred_element_type=jnp.float32) + b_down.astype(jnp.float32)
    return (resid_wide + down_proj).astype(jnp.bfloat16)


def solution(mesh):
    cp_size = mesh.shape["cp"]
    tok_spec = P("dp", ("cp", "sp"), None)
    shift_perm = [(src_idx, (src_idx + 1) % cp_size) for src_idx in range(cp_size)]

    def local_block(hidden, w_qkv, w_out, norm_gain, w_up, b_up, w_down, b_down):
        qkv_proj = jnp.einsum("btc,cjhd->btjhd", hidden, w_qkv, preferred_element_type=jnp.float32).astype(jnp.bfloat16)
        qkv_proj = lax.all_to_all(qkv_proj, "sp", 3, 1, tiled=True)
        q_loc = qkv_proj[:, :, 0]
        k_loc = qkv_proj[:, :, 1]
        v_loc = qkv_proj[:, :, 2]
        batch_size, blk_len, local_heads, head_dim = q_loc.shape
        first_state = attend_step(q_loc, k_loc, v_loc, empty_state(batch_size, local_heads, blk_len, head_dim))

        def pass_step(step_idx, loop_state):
            key_blk, val_blk, soft_state = loop_state
            key_blk, val_blk = lax.ppermute((key_blk, val_blk), "cp", shift_perm)
            return key_blk, val_blk, attend_step(q_loc, key_blk, val_blk, soft_state)

        loop_state = lax.fori_loop(0, cp_size - 1, pass_step, (k_loc, v_loc, first_state))
        final_state = loop_state[2]
        attn_heads = (final_state[2] / final_state[1][..., None]).astype(jnp.bfloat16)
        attn_heads = lax.all_to_all(attn_heads, "sp", 2, 1, tiled=True)
        return block_tail(hidden, attn_heads, w_out, norm_gain, w_up, b_up, w_down, b_down)

    return jax.shard_map(local_block, mesh=mesh, in_specs=(tok_spec, P(), P(), P(), P(), P(), P(), P()), out_specs=tok_spec, check_vma=False)
```

profile of v0, /device:TPU:0, one launch (start us, length us, event | category | flops | bytes accessed | tf_op | source)
XLA Modules:
  0.0 3339.2 jit_solution(6269262413904385205)
XLA Ops:
  0.0 222.7 %fusion.43 = bf16[8,256,3,32,128]{4,1,3,2,0:T(8,128)(2,1)} fusion(bf16[4096,3,32,128]{3,2,1,0:T(8,128)(2,1)} %param.11, bf16[8,256,4096]{2,1,0:T(8,128)(2,1)} %param.10), kind=kOutput, calls=%fused_computation.52 | convolution fusion | flops 206183596032 | bytes 167772160 | tf_op jit(solution)/shard_map/btc,cjhd->btjhd/dot_general | solution.py:41
  222.7 33.7 %copy.16 = bf16[8,256,3,32,128]{4,1,2,0,3:T(8,128)(2,1)} copy(bf16[8,256,3,32,128]{4,1,3,2,0:T(8,128)(2,1)} %fusion.43) | data formatting | bytes 100663296 | tf_op jit(solution)/shard_map/convert_element_type | solution.py:41
  256.4 18.6 all-to-all-start
  275.1 543.3 %all-to-all-done = bf16[8,256,3,32,128]{4,1,2,0,3:T(8,128)(2,1)} async-done(((bf16[8,256,3,32,128]{4,1,2,0,3:T(8,128)(2,1)}), bf16[8,256,3,32,128]{4,1,2,0,3:T(8,128)(2,1)}, u32[]{:S(2)}, u32[]{:S(2)}) %all-to-all-start) | async-done | bytes 50331680 | tf_op jit(solution)/shard_map/all_to_all | solution.py:42
  818.4 33.6 %copy.17 = bf16[8,256,3,2,16,128]{5,1,3,4,0,2:T(8,128)(2,1)} copy(bf16[8,256,3,2,16,128]{5,1,2,0,4,3:T(8,128)(2,1)} %bitcast.3) | data formatting | bytes 100663296 | tf_op jit(solution)/shard_map/all_to_all | solution.py:42
  852.0 56.8 %multiply_reduce_fusion.1 = (f32[8,16,512]{2,1,0:T(8,128)}, f32[8,16,512,512]{2,3,1,0:T(8,128)}) fusion(bf16[8,512,3,16,128]{4,1,3,0,2:T(8,128)(2,1)} %bitcast.73), kind=kOutput, calls=%fused_computation.25 | convolution fusion | flops 8656977920 | bytes 168034304 | tf_op jit(solution)/shard_map/bqhd,bkhd->bhqk/dot_general | solution.py:11
  908.8 32.8 slice_bitcast_fusion
  941.5 41.0 %fusion.22 = f32[8,16,512]{2,1,0:T(8,128)S(1)} fusion(f32[8,16,512,512]{2,3,1,0:T(8,128)} %get-tuple-element.69, f32[8,16,512]{2,1,0:T(8,128)} %get-tuple-element.126), kind=kLoop, calls=%fused_computation.27 | loop fusion | flops 100597760 | bytes 134742016 | tf_op jit(solution)/shard_map/reduce_sum | solution.py:15
  982.6 1.0 exponential_multiply_fusion
  983.6 65.9 %broadcast_add_fusion = f32[8,16,512,128]{3,2,1,0:T(8,128)} fusion(f32[8,16,512]{2,1,0:T(8,128)S(1)} %get-tuple-element.66, f32[8,16,512,512]{2,3,1,0:T(8,128)} %get-tuple-element.69, f32[8,16,512]{2,1,0:T(8,128)} %get-tuple-element.126, bf16[8,512,3,16,128]{4,1,3,0,2:T(8,128)(2,1)} %bitcast.75), kind=kOutput, calls=%fused_computation.59 | convolution fusion | flops 8698986496 | bytes 185073664 | tf_op jit(solution)/shard_map/bhqk,bkhd->bhqd/dot_general | solution.py:16
  1049.5 1345.4 %while.18 = (s32[]{:T(128)}, bf16[8,512,16,128]{3,1,2,0:T(8,128)(2,1)}, bf16[8,512,16,128]{3,1,2,0:T(8,128)(2,1)}, f32[8,16,512]{2,1,0:T(8,128)}, f32[8,16,512]{...) while((s32[]{:T(128)}, ...), condition=%wide.region_5.0_spmd, body=%wide.region_2.0_spmd.sunk | while | flops 17465212928 | bytes 725614784 | solution.py:54
  1049.5 1.8 collective-permute-start.1
  1051.3 180.9 %collective-permute-done = bf16[8,512,16,128]{3,1,2,0:T(8,128)(2,1)} collective-permute-done((bf16[8,512,16,128]{3,1,2,0:T(8,128)(2,1)}, bf16[8,512,16,128]{3,1,2,0:T(8,128)(2,1)}, u32[]{:S(2)}, u32[]{:S(2)}) %collective-permute-start) | collective-permute-done | bytes 16777248 | tf_op jit(solution)/shard_map/while/body/eval_jaxpr/ppermute | solution.py:51
  1232.2 56.1 %multiply_reduce_fusion.3 = (f32[8,16,512]{2,1,0:T(8,128)S(1)}, f32[8,16,512,512]{2,3,1,0:T(8,128)}) fusion(bf16[8,512,16,128]{3,1,2,0:T(8,128)(2,1)} %get-tuple-element.145, bf16[8,512,16,128]{3,1,2,0:T(8,128)(2,1)} %collective-permute-done), kind=kOutput, calls=%fused_computation.1.clone.1 | convolution fusion | flops 8656977920 | bytes 168034304 | tf_op jit(solution)/shard_map/while/body/eval_jaxpr/bqhd,bkhd->bhqk/dot_general | solution.py:11
  1288.3 1.0 max.4
  1289.3 40.9 %fusion.90 = f32[8,16,512]{2,1,0:T(8,128)S(1)} fusion(f32[8,16,512,512]{2,3,1,0:T(8,128)} %get-tuple-element.120, f32[8,16,512]{2,1,0:T(8,128)S(1)} %max.4), kind=kLoop, calls=%fused_computation.3.clone.1 | loop fusion | flops 100597760 | bytes 134742016 | tf_op jit(solution)/shard_map/while/body/eval_jaxpr/reduce_sum | solution.py:15
  1330.3 1.2 multiply_add_fusion.4
  1332.1 14.0 copy.48
  1346.1 65.9 %collective-permute-done.1 = bf16[8,512,16,128]{3,1,2,0:T(8,128)(2,1)} collective-permute-done((bf16[8,512,16,128]{3,1,2,0:T(8,128)(2,1)}, bf16[8,512,16,128]{3,1,2,0:T(8,128)(2,1)}, u32[]{:S(2)}, u32[]{:S(2)}) %collective-permute-start.1) | collective-permute-done | bytes 16777248 | tf_op jit(solution)/shard_map/while/body/eval_jaxpr/ppermute | solution.py:51
  1412.0 13.9 copy.49
  1425.9 72.0 %multiply_add_fusion.5 = f32[8,16,512,128]{3,2,1,0:T(8,128)} fusion(f32[8,16,512,128]{3,2,1,0:T(8,128)} %get-tuple-element.136, f32[8,16,512]{2,1,0:T(8,128)S(1)} %get-tuple-element.122, bf16[8,512,16,128]{3,1,2,0:T(8,128)(2,1)} %collective-permute-done.1, f32[8,16,512,512]{2,3,1,0:T(8,128)} %get-tuple-element.120, f32[8,16,512]{2,1,0:T(8,128)S(1)} %max.4), kind=kOutput, calls=%fused_computation.7.clone.2 | convolution fusion | flops 8707375104 | bytes 218628096 | tf_op jit(solution)/shard_map/while/body/eval_jaxpr/bhqk,bkhd->bhqd/dot_general | solution.py:16
  1497.9 1.8 collective-permute-start.1
  1499.8 180.9 %collective-permute-done = bf16[8,512,16,128]{3,1,2,0:T(8,128)(2,1)} collective-permute-done((bf16[8,512,16,128]{3,1,2,0:T(8,128)(2,1)}, bf16[8,512,16,128]{3,1,2,0:T(8,128)(2,1)}, u32[]{:S(2)}, u32[]{:S(2)}) %collective-permute-start) | collective-permute-done | bytes 16777248 | tf_op jit(solution)/shard_map/while/body/eval_jaxpr/ppermute | solution.py:51
  1680.7 56.1 %multiply_reduce_fusion.3 = (f32[8,16,512]{2,1,0:T(8,128)S(1)}, f32[8,16,512,512]{2,3,1,0:T(8,128)}) fusion(bf16[8,512,16,128]{3,1,2,0:T(8,128)(2,1)} %get-tuple-element.145, bf16[8,512,16,128]{3,1,2,0:T(8,128)(2,1)} %collective-permute-done), kind=kOutput, calls=%fused_computation.1.clone.1 | convolution fusion | flops 8656977920 | bytes 168034304 | tf_op jit(solution)/shard_map/while/body/eval_jaxpr/bqhd,bkhd->bhqk/dot_general | solution.py:11
  1736.8 1.0 max.4
  1737.8 40.9 %fusion.90 = f32[8,16,512]{2,1,0:T(8,128)S(1)} fusion(f32[8,16,512,512]{2,3,1,0:T(8,128)} %get-tuple-element.120, f32[8,16,512]{2,1,0:T(8,128)S(1)} %max.4), kind=kLoop, calls=%fused_computation.3.clone.1 | loop fusion | flops 100597760 | bytes 134742016 | tf_op jit(solution)/shard_map/while/body/eval_jaxpr/reduce_sum | solution.py:15
  1778.7 1.2 multiply_add_fusion.4
  1780.6 14.0 copy.48
  1794.6 65.9 %collective-permute-done.1 = bf16[8,512,16,128]{3,1,2,0:T(8,128)(2,1)} collective-permute-done((bf16[8,512,16,128]{3,1,2,0:T(8,128)(2,1)}, bf16[8,512,16,128]{3,1,2,0:T(8,128)(2,1)}, u32[]{:S(2)}, u32[]{:S(2)}) %collective-permute-start.1) | collective-permute-done | bytes 16777248 | tf_op jit(solution)/shard_map/while/body/eval_jaxpr/ppermute | solution.py:51
  1860.5 13.9 copy.49
  1874.3 72.0 %multiply_add_fusion.5 = f32[8,16,512,128]{3,2,1,0:T(8,128)} fusion(f32[8,16,512,128]{3,2,1,0:T(8,128)} %get-tuple-element.136, f32[8,16,512]{2,1,0:T(8,128)S(1)} %get-tuple-element.122, bf16[8,512,16,128]{3,1,2,0:T(8,128)(2,1)} %collective-permute-done.1, f32[8,16,512,512]{2,3,1,0:T(8,128)} %get-tuple-element.120, f32[8,16,512]{2,1,0:T(8,128)S(1)} %max.4), kind=kOutput, calls=%fused_computation.7.clone.2 | convolution fusion | flops 8707375104 | bytes 218628096 | tf_op jit(solution)/shard_map/while/body/eval_jaxpr/bhqk,bkhd->bhqd/dot_general | solution.py:16
  1946.4 1.8 collective-permute-start.1
  1948.2 180.9 %collective-permute-done = bf16[8,512,16,128]{3,1,2,0:T(8,128)(2,1)} collective-permute-done((bf16[8,512,16,128]{3,1,2,0:T(8,128)(2,1)}, bf16[8,512,16,128]{3,1,2,0:T(8,128)(2,1)}, u32[]{:S(2)}, u32[]{:S(2)}) %collective-permute-start) | collective-permute-done | bytes 16777248 | tf_op jit(solution)/shard_map/while/body/eval_jaxpr/ppermute | solution.py:51
  2129.1 56.1 %multiply_reduce_fusion.3 = (f32[8,16,512]{2,1,0:T(8,128)S(1)}, f32[8,16,512,512]{2,3,1,0:T(8,128)}) fusion(bf16[8,512,16,128]{3,1,2,0:T(8,128)(2,1)} %get-tuple-element.145, bf16[8,512,16,128]{3,1,2,0:T(8,128)(2,1)} %collective-permute-done), kind=kOutput, calls=%fused_computation.1.clone.1 | convolution fusion | flops 8656977920 | bytes 168034304 | tf_op jit(solution)/shard_map/while/body/eval_jaxpr/bqhd,bkhd->bhqk/dot_general | solution.py:11
  2185.2 1.0 max.4
  2186.2 40.9 %fusion.90 = f32[8,16,512]{2,1,0:T(8,128)S(1)} fusion(f32[8,16,512,512]{2,3,1,0:T(8,128)} %get-tuple-element.120, f32[8,16,512]{2,1,0:T(8,128)S(1)} %max.4), kind=kLoop, calls=%fused_computation.3.clone.1 | loop fusion | flops 100597760 | bytes 134742016 | tf_op jit(solution)/shard_map/while/body/eval_jaxpr/reduce_sum | solution.py:15
  2227.2 1.2 multiply_add_fusion.4
  2229.0 14.0 copy.48
  2243.0 65.9 %collective-permute-done.1 = bf16[8,512,16,128]{3,1,2,0:T(8,128)(2,1)} collective-permute-done((bf16[8,512,16,128]{3,1,2,0:T(8,128)(2,1)}, bf16[8,512,16,128]{3,1,2,0:T(8,128)(2,1)}, u32[]{:S(2)}, u32[]{:S(2)}) %collective-permute-start.1) | collective-permute-done | bytes 16777248 | tf_op jit(solution)/shard_map/while/body/eval_jaxpr/ppermute | solution.py:51
  2308.9 13.9 copy.49
  2322.8 72.0 %multiply_add_fusion.5 = f32[8,16,512,128]{3,2,1,0:T(8,128)} fusion(f32[8,16,512,128]{3,2,1,0:T(8,128)} %get-tuple-element.136, f32[8,16,512]{2,1,0:T(8,128)S(1)} %get-tuple-element.122, bf16[8,512,16,128]{3,1,2,0:T(8,128)(2,1)} %collective-permute-done.1, f32[8,16,512,512]{2,3,1,0:T(8,128)} %get-tuple-element.120, f32[8,16,512]{2,1,0:T(8,128)S(1)} %max.4), kind=kOutput, calls=%fused_computation.7.clone.2 | convolution fusion | flops 8707375104 | bytes 218628096 | tf_op jit(solution)/shard_map/while/body/eval_jaxpr/bhqk,bkhd->bhqd/dot_general | solution.py:16
  2395.6 29.6 fusion.42
  2425.2 9.7 all-to-all-start.1
  2436.8 179.8 %all-to-all-done.1 = bf16[8,16,512,128]{3,1,0,2:T(8,128)(2,1)} async-done(((bf16[8,16,512,128]{3,1,0,2:T(8,128)(2,1)}), bf16[8,16,512,128]{3,1,0,2:T(8,128)(2,1)}, u32[]{:S(2)}, u32[]{:S(2)}) %all-to-all-start.1) | async-done | bytes 16777248 | tf_op jit(solution)/shard_map/all_to_all | solution.py:57
  2616.6 16.9 copy.21
  2633.5 79.7 %fusion.36 = (f32[8,256]{1,0:T(8,128)S(1)}, bf16[8,256,4096]{2,1,0:T(8,128)(2,1)}) fusion(bf16[8,32,256,128]{3,2,1,0:T(8,128)(2,1)} %bitcast.76, bf16[32,128,4096]{2,1,0:T(8,128)(2,1)} %param.12, bf16[8,256,4096]{2,1,0:T(8,128)(2,1)} %param.10), kind=kOutput, calls=%fused_computation.42 | convolution fusion | flops 68786585600 | bytes 83894272 | tf_op jit(solution)/shard_map/bhtd,hdc->btc/dot_general | solution.py:25
  2713.2 295.7 %fusion.19 = f32[8,256,16384]{2,1,0:T(8,128)} fusion(bf16[4096,16384]{1,0:T(8,128)(2,1)} %param.14, bf16[8,256,4096]{2,1,0:T(8,128)(2,1)} %get-tuple-element.71, f32[4096]{0:T(1024)S(1)} %copy-done.3, f32[8,256]{1,0:T(8,128)S(1)} %add_rsqrt_fusion), kind=kOutput, calls=%fused_computation.22 | convolution fusion | flops 274911461376 | bytes 285237248 | tf_op jit(solution)/shard_map/btc,cf->btf/dot_general | solution.py:29
  3009.0 329.7 %fusion.39 = bf16[8,256,4096]{2,1,0:T(8,128)(2,1)} fusion(bf16[8,256,4096]{2,1,0:T(8,128)(2,1)} %get-tuple-element.71, f32[4096]{0:T(1024)S(1)} %copy-done.2, bf16[16384,4096]{1,0:T(8,128)(2,1)} %param.16, f32[8,256,16384]{2,1,0:T(8,128)} %fusion.19, f32[16384]{0:T(1024)S(1)} %copy-done), kind=kOutput, calls=%fused_computation.45 | convolution fusion | flops 275247005696 | bytes 302071808 | tf_op jit(solution)/shard_map/btf,fc->btc/dot_general | solution.py:31
  (23 shorter events, 4.7 us)
Async XLA Ops:
  256.4 561.9 %all-to-all-start = ((bf16[8,256,3,32,128]{4,1,2,0,3:T(8,128)(2,1)}), bf16[8,256,3,32,128]{4,1,2,0,3:T(8,128)(2,1)}, u32[]{:S(2)}, u32[]{:S(2)}) async-start(bf16[8,256,3,32,128]{4,1,2,0,3:T(8,128)(2,1)} %copy.16), calls=%async_computation | async-start | bytes 100663296 | tf_op jit(solution)/shard_map/all_to_all | solution.py:42
  1049.5 182.8 %collective-permute-start = (bf16[8,512,16,128]{3,1,2,0:T(8,128)(2,1)}, bf16[8,512,16,128]{3,1,2,0:T(8,128)(2,1)}, u32[]{:S(2)}, u32[]{:S(2)}) collective-permute-start(bf16[8,512,16,128]{3,1,2,0:T(8,128)(2,1)} %get-tuple-element.132), channel_id=1, source_target_pairs={{0,1},{1,2},{2,3},{3,0},{4,5},{5,6},{6,7},{7,4}} | collective-permute-start | bytes 50331656 | tf_op jit(solution)/shard_map/while/body/eval_jaxpr/ppermute | solution.py:51
  1049.5 362.5 %collective-permute-start.1 = (bf16[8,512,16,128]{3,1,2,0:T(8,128)(2,1)}, bf16[8,512,16,128]{3,1,2,0:T(8,128)(2,1)}, u32[]{:S(2)}, u32[]{:S(2)}) collective-permute-start(bf16[8,512,16,128]{3,1,2,0:T(8,128)(2,1)} %get-tuple-element.133), channel_id=1, source_target_pairs={{0,1},{1,2},{2,3},{3,0},{4,5},{5,6},{6,7},{7,4}} | collective-permute-start | bytes 50331656 | tf_op jit(solution)/shard_map/while/body/eval_jaxpr/ppermute | solution.py:51
  1497.9 182.8 %collective-permute-start = (bf16[8,512,16,128]{3,1,2,0:T(8,128)(2,1)}, bf16[8,512,16,128]{3,1,2,0:T(8,128)(2,1)}, u32[]{:S(2)}, u32[]{:S(2)}) collective-permute-start(bf16[8,512,16,128]{3,1,2,0:T(8,128)(2,1)} %get-tuple-element.132), channel_id=1, source_target_pairs={{0,1},{1,2},{2,3},{3,0},{4,5},{5,6},{6,7},{7,4}} | collective-permute-start | bytes 50331656 | tf_op jit(solution)/shard_map/while/body/eval_jaxpr/ppermute | solution.py:51
  1497.9 362.5 %collective-permute-start.1 = (bf16[8,512,16,128]{3,1,2,0:T(8,128)(2,1)}, bf16[8,512,16,128]{3,1,2,0:T(8,128)(2,1)}, u32[]{:S(2)}, u32[]{:S(2)}) collective-permute-start(bf16[8,512,16,128]{3,1,2,0:T(8,128)(2,1)} %get-tuple-element.133), channel_id=1, source_target_pairs={{0,1},{1,2},{2,3},{3,0},{4,5},{5,6},{6,7},{7,4}} | collective-permute-start | bytes 50331656 | tf_op jit(solution)/shard_map/while/body/eval_jaxpr/ppermute | solution.py:51
  1946.4 182.8 %collective-permute-start = (bf16[8,512,16,128]{3,1,2,0:T(8,128)(2,1)}, bf16[8,512,16,128]{3,1,2,0:T(8,128)(2,1)}, u32[]{:S(2)}, u32[]{:S(2)}) collective-permute-start(bf16[8,512,16,128]{3,1,2,0:T(8,128)(2,1)} %get-tuple-element.132), channel_id=1, source_target_pairs={{0,1},{1,2},{2,3},{3,0},{4,5},{5,6},{6,7},{7,4}} | collective-permute-start | bytes 50331656 | tf_op jit(solution)/shard_map/while/body/eval_jaxpr/ppermute | solution.py:51
  1946.4 362.5 %collective-permute-start.1 = (bf16[8,512,16,128]{3,1,2,0:T(8,128)(2,1)}, bf16[8,512,16,128]{3,1,2,0:T(8,128)(2,1)}, u32[]{:S(2)}, u32[]{:S(2)}) collective-permute-start(bf16[8,512,16,128]{3,1,2,0:T(8,128)(2,1)} %get-tuple-element.133), channel_id=1, source_target_pairs={{0,1},{1,2},{2,3},{3,0},{4,5},{5,6},{6,7},{7,4}} | collective-permute-start | bytes 50331656 | tf_op jit(solution)/shard_map/while/body/eval_jaxpr/ppermute | solution.py:51
  2395.6 39.3 %copy-start.4 = (bf16[4096]{0:T(1024)(128)(2,1)S(1)}, bf16[4096]{0:T(1024)(128)(2,1)}, u32[]{:S(2)}) copy-start(bf16[4096]{0:T(1024)(128)(2,1)} %param.13) | copy-start | bytes 24580
  2395.6 39.9 %copy-start.1 = (bf16[16384]{0:T(1024)(128)(2,1)S(1)}, bf16[16384]{0:T(1024)(128)(2,1)}, u32[]{:S(2)}) copy-start(bf16[16384]{0:T(1024)(128)(2,1)} %param.15) | copy-start | bytes 98308
  2395.6 40.5 %copy-start.5 = (bf16[4096]{0:T(1024)(128)(2,1)S(1)}, bf16[4096]{0:T(1024)(128)(2,1)}, u32[]{:S(2)}) copy-start(bf16[4096]{0:T(1024)(128)(2,1)} %param.17) | copy-start | bytes 24580
  2425.2 191.4 %all-to-all-start.1 = ((bf16[8,16,512,128]{3,1,0,2:T(8,128)(2,1)}), bf16[8,16,512,128]{3,1,0,2:T(8,128)(2,1)}, u32[]{:S(2)}, u32[]{:S(2)}) async-start(bf16[8,16,512,128]{3,1,0,2:T(8,128)(2,1)} %fusion.42), calls=%async_computation.1 | async-start | bytes 33554432 | tf_op jit(solution)/shard_map/all_to_all | solution.py:57
  2633.5 79.7 %copy-start.3 = (f32[4096]{0:T(1024)S(1)}, f32[4096]{0:T(1024)}, u32[]{:S(2)}) copy-start(f32[4096]{0:T(1024)} %convert_element_type.53) | copy-start | bytes 49156
  2713.2 295.8 %copy-start = (f32[16384]{0:T(1024)S(1)}, f32[16384]{0:T(1024)}, u32[]{:S(2)}) copy-start(f32[16384]{0:T(1024)} %convert_element_type.55) | copy-start | bytes 196612
  2713.2 295.7 %copy-start.2 = (f32[4096]{0:T(1024)S(1)}, f32[4096]{0:T(1024)}, u32[]{:S(2)}) copy-start(f32[4096]{0:T(1024)} %convert_element_type.57) | copy-start | bytes 49156
where the time goes:
time: 3350 us; the launch traced here: 3340 us
  waiting for transfers between devices  1460 us (44%)
  matrix products  1430 us (43%)
  local copies, waits for them, and re-layouts  204 us (6%)
  other arithmetic  203 us (6%)
  starting transfers between devices  33.8 us (1%)
    ppermute x6, waiting for transfers between devices, pass_step(): key_blk, val_blk = lax.ppermute((key_blk, val_blk), 'cp', shift_perm)  740 us
    all_to_all x1, waiting for transfers between devices, local_block(): qkv_proj = lax.all_to_all(qkv_proj, 'sp', 3, 1, tiled=True)  543 us
    dot_general x1, matrix products, block_tail(): jnp.einsum('btf,fc->btc', up_act, w_down, preferred_element_type=jnp.floa...  330 us
    dot_general x1, matrix products, block_tail(): jnp.einsum('btc,cf->btf', normed, w_up, preferred_element_type=jnp.float32)  296 us
    dot_general x4, matrix products, attend_step(): jnp.einsum('bhqk,bkhd->bhqd', exp_scores.astype(jnp.bfloat16), val_blk, p...  282 us
    dot_general x4, matrix products, attend_step(): jnp.einsum('bqhd,bkhd->bhqk', queries, key_blk, preferred_element_type=jn...  225 us
    dot_general x1, matrix products, local_block(): jnp.einsum('btc,cjhd->btjhd', hidden, w_qkv, preferred_element_type=jnp.f...  223 us
    all_to_all x1, waiting for transfers between devices, local_block(): attn_heads = lax.all_to_all(attn_heads, 'sp', 2, 1, tiled=True)  180 us
  transfers between devices with their start and end apart: 8, of which 8 were waited for; matrix products, arithmetic and copies ran while one was open for 10% of the time, Pallas kernels for 0%

commit v1 on v0

v1 whole, which is shorter than its diff:
```python
import functools
import math

import jax
import jax.numpy as jnp
from jax import lax
from jax.experimental import pallas as pl
from jax.experimental.pallas import tpu as pltpu
from jax.sharding import PartitionSpec as P

NORM_EPS = 1e-6
VMEM_BYTES = 63 * 2**20
BF = jnp.bfloat16
F32 = jnp.float32
ANY = pl.BlockSpec(memory_space=pl.ANY)

ORDER = (0, 2, 4, 1, 6, 3, 5, 7)
PIECES = 8


def peer(rel):
    i, j = lax.axis_index("cp"), lax.axis_index("sp")
    kx, kc, ky = rel // 4, (rel // 2) % 2, rel % 2
    x = lax.rem(i // 2 + kx, 2)
    core = lax.rem(lax.rem(i, 2) + kc, 2)
    cp, sp = x * 2 + core, lax.rem(j + ky, 2)
    return {"cp": cp, "sp": sp}, cp * 2 + sp


def greet():
    bar = pltpu.get_barrier_semaphore()
    for rel in range(1, PIECES):
        pl.semaphore_signal(bar, inc=1, device_id=peer(rel)[0], device_id_type=pl.DeviceIdType.MESH)
    pl.semaphore_wait(bar, PIECES - 1)


def params(**kw):
    return pltpu.CompilerParams(vmem_limit_bytes=VMEM_BYTES, **kw)


def qkv_kernel(hid, w_ref, o_ref, row_out, xs, own_sem, send_sem, recv_sem, out_sem, *, n_tiles, kp):
    t = pl.program_id(0)
    chunk = t // n_tiles

    def send(slot):
        dev, row = peer(ORDER[slot])
        return pltpu.make_async_remote_copy(
            src_ref=hid.at[row], dst_ref=xs.at[slot], send_sem=send_sem.at[slot - 1], recv_sem=recv_sem.at[slot - 1],
            device_id=dev, device_id_type=pl.DeviceIdType.MESH)

    def keep(slot):
        return pltpu.make_async_copy(xs.at[slot], row_out.at[slot], out_sem.at[slot])

    @pl.when(t == 0)
    def _():
        own = pltpu.make_async_copy(hid.at[peer(0)[1]], xs.at[0], own_sem)
        own.start()
        greet()
        for slot in range(1, PIECES):
            send(slot).start()
        own.wait()
        keep(0).start()

    for c in range(PIECES // 2):
        @pl.when(t == c * n_tiles)
        def _(c=c):
            for slot in (2 * c, 2 * c + 1):
                if slot:
                    send(slot).wait_recv()
                    keep(slot).start()

    dim, _, hb, hd = w_ref.shape
    acc = None
    for k in range(0, dim, kp):
        turned = jnp.swapaxes(w_ref[k:k + kp, 0], 0, 1)
        cols = jnp.concatenate([turned[h] for h in range(hb)], axis=1)
        x = xs[pl.ds(2 * chunk, 2), :, k:k + kp]
        d = jnp.dot(x.reshape(-1, kp), cols, preferred_element_type=F32)
        acc = d if acc is None else acc + d
    o_ref[...] = acc.astype(BF)

    @pl.when(t == pl.num_programs(0) - 1)
    def _():
        for slot in range(PIECES):
            if slot:
                send(slot).wait_send()
            keep(slot).wait()


def gather_qkv(hidden, w, hb=8):
    pieces, tok, dim = hidden.shape
    _, kinds, heads, head_dim = w.shape
    per, width, tn = heads // hb, kinds * heads * head_dim, hb * head_dim
    n_tiles = kinds * per
    return pl.pallas_call(
        functools.partial(qkv_kernel, n_tiles=n_tiles, kp=256), name="gather_qkv", grid=(pieces // 2 * n_tiles,),
        in_specs=[ANY, pl.BlockSpec((dim, 1, hb, head_dim), lambda t: (0, t % n_tiles // per, t % per, 0))],
        out_specs=[pl.BlockSpec((2 * tok, tn), lambda t: (t // n_tiles, t % n_tiles)), ANY],
        out_shape=[jax.ShapeDtypeStruct((pieces * tok, width), BF), jax.ShapeDtypeStruct(hidden.shape, BF)],
        scratch_shapes=[pltpu.VMEM(hidden.shape, BF), pltpu.SemaphoreType.DMA, pltpu.SemaphoreType.DMA((pieces - 1,)),
                        pltpu.SemaphoreType.DMA((pieces - 1,)), pltpu.SemaphoreType.DMA((pieces,))],
        compiler_params=params(collective_id=0, has_side_effects=True))(hidden, w)


def attn_kernel(q_ref, k_ref, v_ref, qn_ref, kn_ref, o_ref, ve_ref, sc_ref, *, bq, hd, dim):
    tok = q_ref.shape[0]
    n = tok // bq
    coef = dim ** -0.5 * math.log2(math.e)

    def dot_nt(a, b):
        return lax.dot_general(a, b, (((1,), (1,)), ((), ())), preferred_element_type=F32)

    @pl.when(pl.program_id(0) == 0)
    def _():
        ve_ref[:, dim:] = jnp.zeros((tok, dim), BF)
        sc_ref[...] = dot_nt(q_ref[:bq, :dim], k_ref[:, :dim])

    def scores(g):
        h, i = divmod(g, n)
        if h < hd:
            return dot_nt(q_ref[i * bq:(i + 1) * bq, h * dim:(h + 1) * dim], k_ref[:, h * dim:(h + 1) * dim])
        return dot_nt(qn_ref[...], kn_ref[...])

    s = sc_ref[...]
    for g in range(n * hd):
        h, i = divmod(g, n)
        if i == 0:
            ve_ref[:, :dim] = v_ref[:, h * dim:(h + 1) * dim]
        ahead = scores(g + 1)
        m = jnp.max(s, axis=-1, keepdims=True)
        p = jnp.exp2((s - m) * coef)
        total = jnp.sum(p, axis=-1, keepdims=True)
        o = jnp.dot(p.astype(BF), ve_ref[...], preferred_element_type=F32)
        o_ref[i * bq:(i + 1) * bq, h * dim:(h + 1) * dim] = (o[:, :dim] * (1.0 / total)).astype(BF)
        s = ahead
    sc_ref[...] = s


def attention(qkv, heads, dim, bq=256, hd=2):
    tok = qkv.shape[0]
    steps = heads // hd
    cols = lambda j: pl.BlockSpec((tok, hd * dim), lambda t: (0, j * steps + t))
    ahead = lambda t: jnp.minimum((t + 1) * hd, heads - 1)
    return pl.pallas_call(
        functools.partial(attn_kernel, bq=bq, hd=hd, dim=dim), name="attention", grid=(steps,),
        in_specs=[cols(0), cols(1), cols(2), pl.BlockSpec((bq, dim), lambda t: (0, ahead(t))),
                  pl.BlockSpec((tok, dim), lambda t: (0, heads + ahead(t)))],
        out_specs=pl.BlockSpec((tok, hd * dim), lambda t: (0, t)),
        out_shape=jax.ShapeDtypeStruct((tok, heads * dim), BF),
        scratch_shapes=[pltpu.VMEM((tok, 2 * dim), BF), pltpu.VMEM((bq, tok), F32)],
        compiler_params=params())(*[qkv] * 5)


TANH_LIN = math.sqrt(2 / math.pi)
TANH_CUB = TANH_LIN * 0.044715


def gelu(z):
    half = 0.5 * z
    return half + half * jnp.tanh(z * (TANH_LIN + TANH_CUB * (z * z)))


def up_kernel(r_hbm, g_ref, w_ref, b_ref, o_ref, xn, rbuf, z0, z1, sem, *, tm, tn, sub, kp, ep):
    t = pl.program_id(0)
    tok, dim = xn.shape
    nm, last = tok // tm, pl.num_programs(0) - 1
    rc = rbuf.shape[1]

    @pl.when(t == 0)
    def _():
        fetch = lambda i: pltpu.make_async_copy(r_hbm.at[pl.ds(i * rc, rc)], rbuf.at[i % 2], sem.at[i % 2])
        fetch(0).start()
        gain = g_ref[...].astype(F32)
        for i in range(tok // rc):
            if i + 1 < tok // rc:
                fetch(i + 1).start()
            fetch(i).wait()

            def rows(u, _, i=i):
                at = pl.multiple_of(u * 32, 32)
                x = rbuf[i % 2, pl.ds(at, 32), :].astype(F32)
                inv = lax.rsqrt(jnp.mean(x * x, axis=-1, keepdims=True) + NORM_EPS)
                xn[pl.ds(pl.multiple_of(i * rc + at, 32), 32), :] = (x * inv * gain).astype(BF)
                return 0

            lax.fori_loop(0, rc // 32, rows, 0)

    col = jnp.maximum((t - 1) // nm, 0) * tn
    bias = lambda: b_ref[:, pl.ds(pl.multiple_of(col, tn), tn)].astype(F32)

    def tile(z_now, z_prev):
        base = pl.multiple_of(lax.rem(t, nm) * tm, tm)
        b = bias()
        parts = [(e, c) for e in range(0, tm, ep) for c in range(0, tn, sub)]
        share = len(parts) / (tm // sub * (tn // sub) * (dim // kp))
        done = step = 0
        for c in range(0, tn, sub):
            for r in range(0, tm, sub):
                acc = None
                for k in range(0, dim, kp):
                    d = jnp.dot(xn[pl.ds(base + r, sub), k:k + kp], w_ref[k:k + kp, c:c + sub], preferred_element_type=F32)
                    acc = d if acc is None else acc + d
                    step += 1
                    while done < step * share - 1e-9:
                        e, ec = parts[done]
                        done += 1
                        o_ref[e:e + ep, ec:ec + sub] = gelu(z_prev[e:e + ep, ec:ec + sub] + b[:, ec:ec + sub]).astype(BF)
                z_now[r:r + sub, c:c + sub] = acc

    for par, (za, zb) in enumerate(((z0, z1), (z1, z0))):
        @pl.when((t < last) & (lax.rem(t, 2) == par))
        def _(za=za, zb=zb):
            tile(za, zb)

    @pl.when(t == last)
    def _():
        o_ref[...] = gelu(z1[...] + bias()).astype(BF)


def norm_up(resid, gain, w, b, tm=1024, tn=1024):
    tok, dim = resid.shape
    nm = tok // tm
    tiles = nm * (w.shape[1] // tn)
    prev = lambda t: jnp.maximum(t - 1, 0)
    return pl.pallas_call(
        functools.partial(up_kernel, tm=tm, tn=tn, sub=512, kp=256, ep=32), name="norm_up", grid=(tiles + 1,),
        in_specs=[ANY, pl.BlockSpec((1, dim), lambda t: (0, 0)),
                  pl.BlockSpec((dim, tn), lambda t: (0, jnp.minimum(t, tiles - 1) // nm)),
                  pl.BlockSpec((1, w.shape[1]), lambda t: (0, 0))],
        out_specs=pl.BlockSpec((tm, tn), lambda t: (prev(t) % nm, prev(t) // nm)),
        out_shape=jax.ShapeDtypeStruct((tok, w.shape[1]), BF),
        scratch_shapes=[pltpu.VMEM((tok, dim), BF), pltpu.VMEM((2, 256, dim), BF), pltpu.VMEM((tm, tn), F32),
                        pltpu.VMEM((tm, tn), F32), pltpu.SemaphoreType.DMA((2,))],
        compiler_params=params())(resid, gain, w, b)


SLOTS = 4


def down_kernel(a_ref, w_ref, r_ref, b_ref, out, acc, obuf, own_sem, send_sem, recv_sem, *, tn, nk, nn):
    t = pl.program_id(0)
    half = PIECES // 2
    tiles = 2 * nn
    q, k = t // nk, lax.rem(t, nk)
    tok = out.shape[1]

    def moves(tile):
        far = tile < nn
        slots = range(half, PIECES) if far else range(half)
        cols = pl.ds((tile % nn) * tn, tn)
        my_row = peer(0)[1]
        for p, slot in enumerate(slots):
            src = obuf.at[tile % SLOTS, pl.ds(p * tok, tok)]
            if slot == 0:
                yield pltpu.make_async_copy(src, out.at[my_row, :, cols], own_sem.at[tile % nn]), None
            else:
                yield None, pltpu.make_async_remote_copy(
                    src_ref=src, dst_ref=out.at[my_row, :, cols], send_sem=send_sem.at[tile, p],
                    recv_sem=recv_sem.at[tile % nn, slot - 1], device_id=peer(ORDER[slot])[0],
                    device_id_type=pl.DeviceIdType.MESH)

    @pl.when(t == 0)
    def _():
        greet()

    for tile in range(tiles):
        @pl.when(t == (tile + 1) * nk)
        def _(tile=tile):
            for local, remote in moves(tile):
                (local or remote).start()

        if tile + SLOTS < tiles:
            @pl.when(t == (tile + SLOTS) * nk + nk - 1)
            def _(tile=tile):
                for local, remote in moves(tile):
                    if remote:
                        remote.wait_send()
                    else:
                        local.wait()

    @pl.when(q < tiles)
    def _():
        @pl.when(k == 0)
        def _():
            acc[...] = jnp.dot(a_ref[...], w_ref[...], preferred_element_type=F32)

        @pl.when((k > 0) & (k < nk - 1))
        def _():
            acc[...] += jnp.dot(a_ref[...], w_ref[...], preferred_element_type=F32)

        @pl.when(k == nk - 1)
        def _():
            d = jnp.dot(a_ref[...], w_ref[...], preferred_element_type=F32)
            y = r_ref[...].astype(F32) + ((acc[...] + d) + b_ref[...].astype(F32))
            obuf[lax.rem(q, SLOTS)] = y.astype(BF)

    @pl.when(q == tiles)
    def _():
        for tile in range(tiles):
            for local, remote in moves(tile):
                if tile + SLOTS >= tiles:
                    if remote:
                        remote.wait_send()
                    else:
                        local.wait()
                if remote:
                    remote.wait_recv()


def down_scatter(act, w, resid, b, tok, tn=1024, tk=4096):
    rows, kdim = act.shape
    tm, dim = rows // 2, w.shape[1]
    nn, nk = dim // tn, kdim // tk
    tiles = 2 * nn
    cur = lambda t: jnp.minimum(t, tiles * nk - 1)
    m_of = lambda t: 1 - cur(t) // (nk * nn)
    n_of = lambda t: (cur(t) // nk) % nn
    return pl.pallas_call(
        functools.partial(down_kernel, tn=tn, nk=nk, nn=nn), name="down_scatter", grid=(tiles * nk + 1,),
        in_specs=[pl.BlockSpec((tm, tk), lambda t: (m_of(t), cur(t) % nk)),
                  pl.BlockSpec((tk, tn), lambda t: (cur(t) % nk, n_of(t))),
                  pl.BlockSpec((tm, tn), lambda t: (m_of(t), n_of(t))), pl.BlockSpec((1, tn), lambda t: (0, n_of(t)))],
        out_specs=ANY, out_shape=jax.ShapeDtypeStruct((PIECES, tok, dim), BF),
        scratch_shapes=[pltpu.VMEM((tm, tn), F32), pltpu.VMEM((SLOTS, tm, tn), BF), pltpu.SemaphoreType.DMA((nn,)),
                        pltpu.SemaphoreType.DMA((tiles, PIECES // 2)), pltpu.SemaphoreType.DMA((nn, PIECES - 1))],
        compiler_params=params(collective_id=1, has_side_effects=True))(act, w, resid, b)


def solution(mesh):
    tok_spec = P("dp", ("cp", "sp"), None)

    def local_block(hidden, w_qkv, w_out, norm_gain, w_up, b_up, w_down, b_down):
        pieces, tok, dim = hidden.shape
        _, _, heads, head_dim = w_qkv.shape
        qkv, row = gather_qkv(hidden, w_qkv)
        attn = attention(qkv, heads, head_dim)
        attn_out = jnp.dot(attn, w_out.reshape(heads * head_dim, dim), preferred_element_type=F32).astype(BF)
        resid = (row.reshape(pieces * tok, dim).astype(F32) + attn_out.astype(F32)).astype(BF)
        act = norm_up(resid, norm_gain.reshape(1, dim), w_up, b_up.reshape(1, -1))
        return down_scatter(act, w_down, resid, b_down.reshape(1, dim), tok)

    return jax.shard_map(local_block, mesh=mesh, in_specs=(tok_spec, P(), P(), P(), P(), P(), P(), P()), out_specs=tok_spec, check_vma=False)
```

time: 3350 us -> 1140 us (0.34)
  waiting for transfers between devices: 1460 us -> 0 us
  matrix products: 1430 us -> 80.6 us
  Pallas kernels: 0 us -> 1040 us
  other arithmetic: 203 us -> 0 us
  local copies, waits for them, and re-layouts: 204 us -> 18.1 us
  starting transfers between devices: 33.8 us -> 0 us
    dot_general x12 -> x1, matrix products: 1430 us -> 80.6 us  [local_block(): jnp.dot(attn, w_out.reshape(heads * head_dim, dim), preferred_element_typ...]
    pallas_call x0 -> x4, Pallas kernels: none -> 1040 us  [the longest x1 316 us: norm_up(): pl.pallas_call(functools.partial(up_kernel, tm=tm, tn=tn, sub=512, kp=256...]
    ppermute x6 -> x0, waiting for transfers between devices: 740 us -> none  [pass_step(): key_blk, val_blk = lax.ppermute((key_blk, val_blk), 'cp', shift_perm)]
    all_to_all x2 -> x0, waiting for transfers between devices: 723 us -> none  [the longest x1 543 us: local_block(): qkv_proj = lax.all_to_all(qkv_proj, 'sp', 3, 1, tiled=True)]
    reduce_sum x4 -> x0, other arithmetic: 164 us -> none  [attend_step(): new_sum = run_sum * rescale + jnp.sum(exp_scores, axis=-1)]
    while x10 -> x0, local copies, waits for them, and re-layouts: 86.5 us -> none
    all_to_all x2 -> x0, local copies, waits for them, and re-layouts: 50.5 us -> none  [the longest x1 33.6 us: local_block(): qkv_proj = lax.all_to_all(qkv_proj, 'sp', 3, 1, tiled=True)]
    convert_element_type x1 -> x0, local copies, waits for them, and re-layouts: 33.7 us -> none  [local_block(): jnp.einsum('btc,cjhd->btjhd', hidden, w_qkv, preferred_element_type=jnp.f...]
  transfers between devices with their start and end apart: 8 -> 0, of which waited for: 8 -> 0; matrix products, arithmetic and copies ran while one was open for 10% -> 0% of each run, Pallas kernels for 0% -> 0%
where the time goes in v1:
time: 1140 us
  Pallas kernels  1040 us (91%)
  matrix products  80.6 us (7%)
  local copies, waits for them, and re-layouts  18.1 us (2%)
    pallas_call x1, Pallas kernels, norm_up(): pl.pallas_call(functools.partial(up_kernel, tm=tm, tn=tn, sub=512, kp=256...  316 us
    pallas_call x1, Pallas kernels, down_scatter(): pl.pallas_call(functools.partial(down_kernel, tn=tn, nk=nk, nn=nn), name=...  311 us
    pallas_call x1, Pallas kernels, gather_qkv(): pl.pallas_call(functools.partial(qkv_kernel, n_tiles=n_tiles, kp=256), na...  246 us
    pallas_call x1, Pallas kernels, attention(): pl.pallas_call(functools.partial(attn_kernel, bq=bq, hd=hd, dim=dim), nam...  166 us
    dot_general x1, matrix products, local_block(): jnp.dot(attn, w_out.reshape(heads * head_dim, dim), preferred_element_typ...  80.6 us

profile of v1, /device:TPU:0, one launch (start us, length us, event | category | flops | bytes accessed | tf_op | source)
XLA Modules:
  0.0 1137.4 jit_solution(3928645539170538192)
XLA Ops:
  0.0 1.3 reshape.16.g_ref
  1.3 1.3 reshape.18.b_ref
  2.6 1.4 reshape.17.b_ref
  4.0 245.5 %gather_qkv.1 = (bf16[2048,12288]{1,0:T(8,128)(2,1)}, bf16[8,256,4096]{2,1,0:T(8,128)(2,1)}) custom-call(bf16[8,256,4096]{2,1,0:T(8,128)(2,1)} %hid.1, bf16[4096,3,32,128]{3,2,1,0:T(8,128)(2,1)} %w_ref.3), custom_call_target="tpu_custom_call" | custom-call | tf_op jit(solution)/shard_map/gather_qkv/pallas_call | solution.py:95
  249.6 165.9 %attention.1 = bf16[2048,4096]{1,0:T(8,128)(2,1)} custom-call(bf16[2048,12288]{1,0:T(8,128)(2,1)} %get-tuple-element.8.q_ref.k_ref.v_ref.qn_ref.kn_ref, bf16[2048,12288]{1,0:T(8,128)(2,1)} %get-tuple-element.8.q_ref.k_ref.v_ref.qn_ref.kn_ref, bf16[2048,12288]{1,0:T(8,128)(2,1)} %get-tuple-element.8.q_ref.k_ref.v_ref.qn_ref.kn_ref, ...), custom_call_target="tpu_custom_call" | custom-call | tf_op jit(solution)/shard_map/attention/pallas_call | solution.py:144
  415.5 80.6 %fusion.r_hbm.r_ref = bf16[2048,4096]{1,0:T(8,128)(2,1)} fusion(bf16[8,256,4096]{2,1,0:T(8,128)(2,1)} %get-tuple-element.7, bf16[2048,4096]{1,0:T(8,128)(2,1)} %attention.1, bf16[4096,4096]{1,0:T(8,128)(2,1)} %bitcast.6), kind=kOutput, calls=%fused_computation.1 | convolution fusion | flops 68761419776 | bytes 83886080 | tf_op jit(solution)/shard_map/dot_general | solution.py:337
  496.1 315.8 %norm_up.1.a_ref = bf16[2048,16384]{1,0:T(8,128)(2,1)} custom-call(bf16[2048,4096]{1,0:T(8,128)(2,1)} %fusion.r_hbm.r_ref, bf16[1,4096]{1,0:T(2,128)(2,1)} %reshape.16.g_ref, bf16[4096,16384]{1,0:T(8,128)(2,1)} %w_ref.4, bf16[1,16384]{1,0:T(2,128)(2,1)} %reshape.17.b_ref), custom_call_target="tpu_custom_call" | custom-call | tf_op jit(solution)/shard_map/norm_up/pallas_call | solution.py:225
  812.0 311.0 %down_scatter.1 = bf16[8,256,4096]{2,1,0:T(8,128)(2,1)} custom-call(bf16[2048,16384]{1,0:T(8,128)(2,1)} %norm_up.1.a_ref, bf16[16384,4096]{1,0:T(8,128)(2,1)} %w_ref.5, bf16[2048,4096]{1,0:T(8,128)(2,1)} %fusion.r_hbm.r_ref, bf16[1,4096]{1,0:T(2,128)(2,1)} %reshape.18.b_ref), custom_call_target="tpu_custom_call" | custom-call | tf_op jit(solution)/shard_map/down_scatter/pallas_call | solution.py:318
  1123.0 14.1 %copy.10 = bf16[8,256,4096]{2,1,0:T(8,128)(2,1)} copy(bf16[8,256,4096]{2,1,0:T(8,128)(2,1)} %down_scatter.1) | data formatting | bytes 33554432
